TPU v7x, 32 devices: a whole 2x2x4 slice. The times are simulated.
32 devices in a mesh: blk: 16 (over z, y, core), dp: 2 (over x).
Axes of the slice: x: 2, y: 2, z: 4, core: 2. Of those that a mesh axis runs over, the one named last changes fastest.
Arguments:
- query_feats: bfloat16 [2, 6144, 1024], P('dp', 'blk'), may hold values from -12 to 12
- item_feats: bfloat16 [2, 6144, 1024], P('dp', 'blk'), may hold values from -12 to 12
- item_ids: int32 [2, 6144], P('dp', 'blk'), may hold values from 0 to 1048575
- bucket_ids: int32 [2, 6144], P('dp', 'blk'), may hold values from 0 to 255
- bucket_logq: float32 [256], replicated, may hold values from -7 to -5.5
- query_tower: bfloat16 [1024, 256], replicated, may hold values from -0.1875 to 0.1875
- item_tower: bfloat16 [1024, 256], replicated, may hold values from -0.1875 to 0.1875
Outputs:
- grad_query_tower: float32 [1024, 256], replicated
- grad_item_tower: float32 [1024, 256], replicated
- loss: float32 [], replicated
All inputs are finite; a program needn't handle non-finite values.
Results may differ from a plain program's by a relative error of at most 0.0041.
Values may be sent and summed in bfloat16 or wider, within the bound.
A program may use at most 128 MiB of HBM per device.

v0:
```python
import math

import jax
import jax.numpy as jnp
from jax import lax
from jax.sharding import PartitionSpec as P

EXCLUDED = -1e30


def contract_last(left, right):
    return lax.dot_general(
        left, right, (((1,), (1,)), ((), ())), preferred_element_type=jnp.float32
    )


def contract_first(left, right):
    return lax.dot_general(
        left, right, (((0,), (0,)), ((), ())), preferred_element_type=jnp.float32
    )


def on_device(query_feats, item_feats, item_ids, bucket_ids, bucket_logq, query_tower, item_tower):
    query_input = query_feats[0]
    item_input = item_feats[0]
    own_ids = item_ids[0]
    local_rows = query_input.shape[0]
    embed_width = query_tower.shape[1]
    scaling = 1.0 / math.sqrt(embed_width)
    query_vecs = jnp.dot(query_input, query_tower, preferred_element_type=jnp.float32).astype(
        jnp.bfloat16
    )
    item_vecs = jnp.dot(item_input, item_tower, preferred_element_type=jnp.float32).astype(
        jnp.bfloat16
    )
    all_items = lax.all_gather(item_vecs, "blk", axis=0, tiled=True)
    all_ids, all_buckets = (
        lax.all_gather(own_ids, "blk", axis=0, tiled=True),
        lax.all_gather(bucket_ids[0], "blk", axis=0, tiled=True),
    )
    group_size = all_ids.shape[0]
    bucket_range = jnp.arange(bucket_logq.shape[0], dtype=jnp.int32)
    correction = jnp.sum(
        jnp.where(all_buckets[:, None] == bucket_range[None, :], bucket_logq[None, :], 0.0), axis=1
    )
    offset = lax.axis_index("blk") * local_rows
    rows_global = offset + jnp.arange(local_rows, dtype=jnp.int32)
    columns = jnp.arange(group_size, dtype=jnp.int32)
    scores = contract_last(query_vecs, all_items) * scaling - correction[None, :]
    duplicate = (all_ids[None, :] == own_ids[:, None]) & (columns[None, :] != rows_global[:, None])
    masked = jnp.where(duplicate, EXCLUDED, scores)
    peaks = jnp.max(masked, axis=1)
    log_total = peaks + jnp.log(jnp.sum(jnp.exp(masked - peaks[:, None]), axis=1))
    softmax = jnp.exp(masked - log_total[:, None]).astype(jnp.bfloat16)
    positive = jnp.diagonal(lax.dynamic_slice_in_dim(scores, offset, local_rows, 1))
    loss_local = jnp.sum(log_total - positive)
    query_grad = (
        (
            jnp.dot(softmax, all_items, preferred_element_type=jnp.float32)
            - item_vecs.astype(jnp.float32)
        )
        * scaling
    ).astype(jnp.bfloat16)
    tower_query = contract_first(query_input, query_grad)
    all_totals = lax.all_gather(log_total, "blk", axis=0, tiled=True)
    own_correction = lax.dynamic_slice_in_dim(correction, offset, local_rows, 0)
    shard_rows = lax.all_gather(query_vecs, "blk", axis=0, tiled=True)
    row_count = shard_rows.shape[0]
    piece_rows = jnp.arange(row_count, dtype=jnp.int32)
    piece_scores = contract_last(shard_rows, item_vecs) * scaling - own_correction[None, :]
    piece_dup = (own_ids[None, :] == all_ids[:, None]) & (
        rows_global[None, :] != piece_rows[:, None]
    )
    piece_masked = jnp.where(piece_dup, EXCLUDED, piece_scores)
    piece_soft = jnp.exp(piece_masked - all_totals[:, None]).astype(jnp.bfloat16)
    item_sums = contract_first(piece_soft, shard_rows)
    item_grad = ((item_sums - query_vecs.astype(jnp.float32)) * scaling).astype(jnp.bfloat16)
    tower_item = contract_first(item_input, item_grad)
    grad_query, grad_item, loss_total = lax.psum(
        (tower_query, tower_item, loss_local), ("blk", "dp")
    )
    loss = loss_total / (lax.axis_size("dp") * group_size)
    return (grad_query, grad_item, loss)


def solution(mesh):
    return jax.shard_map(
        on_device,
        mesh=mesh,
        in_specs=(
            P("dp", "blk", None),
            P("dp", "blk", None),
            P("dp", "blk"),
            P("dp", "blk"),
            P(),
            P(),
            P(),
        ),
        out_specs=(P(), P(), P()),
        check_vma=False,
    )
```

profile of v0, /device:TPU:1, one launch (start us, length us, event | category | flops | bytes accessed | tf_op | source)
XLA Modules:
  0.0 269.4 jit_solution(16974433415751441784)
XLA Ops:
  7.2 0.0 copy-start
  7.2 0.0 all-gather.6.cloned.1.call-start
  7.2 1.1 copy-done
  8.3 2.1 convolution_convert_fusion
  10.4 0.0 all-gather.6.cloned.1.call-update
  10.4 0.0 all-gather.8.cloned.1.call-start
  10.5 2.3 convolution_convert_fusion.1
  12.8 0.0 all-gather.8.cloned.1.call-update
  12.8 0.0 all-reduce.3.cloned.1.call-start
  12.9 0.7 reduce
  13.6 23.3 %all-gather.1 = s32[1,6144]{1,0:T(1,128)S(1)} all-gather(s32[1,384]{1,0:T(1,128)} %param.10), channel_id=3, replica_groups=mesh['blk'=16,'dp'=2] {'blk'}, dimensions={1}, use_global_device_ids=true | all-gather | bytes 26112 | tf_op jit(solution)/shard_map/all_gather | solution.py:39
  36.9 4.4 %select_reduce_fusion = f32[6144]{0:T(1024)S(1)} fusion(f32[256]{0:T(256)} %param.11, s32[6144]{0:T(1024)S(1)} %bitcast.30), kind=kLoop, calls=%fused_computation.10 | loop fusion | flops 4712448 | bytes 50176 | tf_op jit(solution)/shard_map/reduce_sum | solution.py:43
  41.2 0.1 dynamic_slice.6
  41.4 18.0 %all-gather = s32[1,6144]{1,0:T(1,128)S(1)} all-gather(s32[1,384]{1,0:T(1,128)} %param.9), channel_id=2, replica_groups=mesh['blk'=16,'dp'=2] {'blk'}, dimensions={1}, use_global_device_ids=true | all-gather | bytes 26112 | tf_op jit(solution)/shard_map/all_gather | solution.py:38
  59.4 0.0 all-gather.6.cloned.1.call-done
  59.4 5.1 %fusion.3 = (f32[384]{0:T(512)S(1)}, f32[384,6144]{1,0:T(8,128)S(1)}) fusion(s32[384]{0:T(512)S(1)} %iota_add_fusion, s32[6144]{0:T(1024)S(1)} %bitcast.26, s32[384]{0:T(512)S(1)} %reduce, f32[6144]{0:T(1024)S(1)} %select_reduce_fusion, bf16[384,256]{1,0:T(8,128)(2,1)} %convolution_convert_fusion.1, bf16[6144,256]{1,0:T(8,128)(2,1)} %all-gather.6.cloned.1.call-done), kind=kOutput, calls=%fused_computation.12 | convolution fusion | flops 1224474240 | bytes 12833280 | tf_op jit(solution)/shard_map/dot_general | solution.py:12
  64.4 0.0 copy-start.1
  64.4 0.0 copy-start.3
  64.5 0.0 copy-start.4
  64.5 3.6 %copy-done.1 = f32[384,6144]{1,0:T(8,128)} copy-done((f32[384,6144]{1,0:T(8,128)}, f32[384,6144]{1,0:T(8,128)S(1)}, u32[]{:S(2)}) %copy-start.1) | copy-done | bytes 9437208
  68.1 0.1 constant_dynamic-slice_fusion
  68.1 3.4 %gather_fusion = f32[384]{0:T(512)S(1)} fusion(f32[384,384]{1,0:T(8,128)S(1)} %constant_dynamic-slice_fusion, s32[384]{0:T(512)S(1)} %or_reduce_fusion), kind=kCustom, calls=%fused_computation | custom fusion | bytes 6144 | tf_op jit(solution)/shard_map/jit(diagonal)/cond/branch_0_fun/gather | solution.py:55
  71.6 6.0 %exponential_reduce_fusion = f32[384]{0:T(512)S(1)} fusion(f32[384,6144]{1,0:T(8,128)} %copy-done.1, f32[384]{0:T(512)S(1)} %get-tuple-element.19, s32[384]{0:T(512)S(1)} %iota_add_fusion, s32[6144]{0:T(1024)S(1)} %bitcast.27, s32[384]{0:T(512)S(1)} %reduce), kind=kLoop, calls=%fused_computation.4 | loop fusion | flops 14155392 | bytes 9467904 | tf_op jit(solution)/shard_map/reduce_sum | solution.py:53
  77.6 0.6 subtract_reduce_fusion
  78.2 19.5 %all-gather.2 = f32[16,1,384]{2,1,0:T(1,128)S(1)} all-gather(f32[1,1,384]{2,1,0:T(1,128)S(1)} %reshape.37), channel_id=1, replica_groups=mesh['blk'=16,'dp'=2] {'blk'}, dimensions={0}, use_global_device_ids=true | all-gather | bytes 26112 | tf_op jit(solution)/shard_map/all_gather | solution.py:65
  97.7 8.0 %all-gather.8.cloned.1.call-done = bf16[6144,256]{1,0:T(8,128)(2,1)} async-done(((bf16[384,256]{1,0:T(8,128)(2,1)}), bf16[6144,256]{1,0:T(8,128)(2,1)}) %all-gather.8.cloned.1.call-update) | async-done | bytes 3145744 | tf_op jit(solution)/shard_map/all_gather | solution.py:67
  105.7 0.0 copy-done.3
  105.7 0.0 copy-done.4
  105.7 0.0 copy-start.2
  105.7 8.5 %fusion.11 = bf16[384,256]{1,0:T(8,128)(2,1)S(1)} fusion(bf16[6144,256]{1,0:T(8,128)(2,1)} %all-gather.8.cloned.1.call-done, bf16[384,256]{1,0:T(8,128)(2,1)S(1)} %copy-done.3, f32[6144]{0:T(1024)S(1)} %bitcast.31, f32[384]{0:T(512)S(1)} %dynamic_slice.6, s32[384]{0:T(512)S(1)} %iota_add_fusion, s32[384]{0:T(512)S(1)} %reduce, s32[6144]{0:T(1024)S(1)} %bitcast.28, ...), kind=kOutput, calls=%fused_computation.24 | convolution fusion | flops 2435186688 | bytes 3789312 | tf_op jit(solution)/shard_map/dot_general | solution.py:18
  114.1 1.4 convolution_bitcast_fusion
  115.6 0.0 copy-done.2
  115.6 9.0 %convolution_bitcast_fusion.1 = f32[1024,256]{0,1:T(8,128)} fusion(bf16[6144,256]{1,0:T(8,128)(2,1)} %all-gather.6.cloned.1.call-done, f32[384,6144]{1,0:T(8,128)} %copy-done.1, f32[384]{0:T(512)S(1)} %get-tuple-element.18, s32[384]{0:T(512)S(1)} %iota_add_fusion, s32[6144]{0:T(1024)S(1)} %bitcast.29, s32[384]{0:T(512)S(1)} %reduce, ...), kind=kOutput, calls=%fused_computation.16 | convolution fusion | flops 1423835136 | bytes 14643712 | tf_op jit(solution)/shard_map/dot_general | solution.py:18
  124.6 0.0 all-reduce.3.cloned.1.call-update
  124.6 39.4 %psum.23 = f32[]{:T(128)} all-reduce(f32[]{:T(128)} %get-tuple-element.17), channel_id=1, replica_groups=mesh['blk'=16,'dp'=2] {'blk','dp'}, use_global_device_ids=true, to_apply=%region_6.7 | all-reduce | flops 1 | bytes 8 | tf_op jit(solution)/shard_map/psum | solution.py:79
  164.6 92.0 %all-reduce.3.cloned.1.call-done = (f32[1024,256]{0,1:T(8,128)}, f32[1024,256]{0,1:T(8,128)}) async-done(((f32[1024,256]{0,1:T(8,128)}, f32[1024,256]{0,1:T(8,128)}), (f32[1024,256]{0,1:T(8,128)}, f32[1024,256]{0,1:T(8,128)})) %all-reduce.3.cloned.1.call-update) | async-done | bytes 2097168 | tf_op jit(solution)/shard_map/psum | solution.py:79
  256.7 2.5 copy.16
  259.2 2.5 copy.17
  (3 shorter events, 0.0 us)
Async XLA Ops:
  7.2 1.1 copy-start
  7.2 52.2 %all-gather.6.cloned.1.call-start = ((), (), s32[]{:S(2)}) async-start(), calls=%async_computation | async-start | bytes 3342336 | tf_op jit(solution)/shard_map/all_gather | solution.py:36
  10.4 95.3 %all-gather.8.cloned.1.call-start = ((), (), s32[]{:S(2)}) async-start(), calls=%async_computation.1 | async-start | bytes 3342336 | tf_op jit(solution)/shard_map/all_gather | solution.py:67
  12.8 243.8 %all-reduce.3.cloned.1.call-start = ((), (), s32[]{:S(2)}) async-start(), calls=%async_computation.2 | async-start | bytes 4194304 | tf_op jit(solution)/shard_map/psum | solution.py:79
  64.4 3.6 %copy-start.1 = (f32[384,6144]{1,0:T(8,128)}, f32[384,6144]{1,0:T(8,128)S(1)}, u32[]{:S(2)}) copy-start(f32[384,6144]{1,0:T(8,128)S(1)} %get-tuple-element.20) | copy-start | bytes 28311556
  64.4 41.2 %copy-start.3 = (bf16[384,256]{1,0:T(8,128)(2,1)S(1)}, bf16[384,256]{1,0:T(8,128)(2,1)}, u32[]{:S(2)}) copy-start(bf16[384,256]{1,0:T(8,128)(2,1)} %convolution_convert_fusion) | copy-start | bytes 589828
  64.5 41.2 %copy-start.4 = (bf16[384,256]{1,0:T(8,128)(2,1)S(1)}, bf16[384,256]{1,0:T(8,128)(2,1)}, u32[]{:S(2)}) copy-start(bf16[384,256]{1,0:T(8,128)(2,1)} %convolution_convert_fusion.1) | copy-start | bytes 589828
  105.7 9.9 %copy-start.2 = (bf16[1,384,1024]{2,1,0:T(8,128)(2,1)S(1)}, bf16[1,384,1024]{2,1,0:T(8,128)(2,1)}, u32[]{:S(2)}) copy-start(bf16[1,384,1024]{2,1,0:T(8,128)(2,1)} %param.7) | copy-start | bytes 2359300
Sparse Core Ops, SparseCore 0:
  10.8 47.9 all-gather.5
  61.7 43.8 all-gather.7
  124.7 131.8 all-reduce.2
where the time goes:
time: 272 us; the launch traced here: 269 us
  waiting for transfers between devices  100 us (37%)
  blocking collectives  100 us (37%)
  matrix products  28.4 us (10%)
  between operations  15.6 us (6%)
  local copies, waits for them, and re-layouts  13.3 us (5%)
  other arithmetic  11.7 us (4%)
    psum x1, waiting for transfers between devices, on_device(): lax.psum((tower_query, tower_item, loss_local), ('blk', 'dp'))  92 us
    psum x1, blocking collectives, on_device(): lax.psum((tower_query, tower_item, loss_local), ('blk', 'dp'))  39.4 us
    all_gather x1, blocking collectives, on_device(): lax.all_gather(bucket_ids[0], 'blk', axis=0, tiled=True)  23.3 us
    all_gather x1, blocking collectives, on_device(): all_totals = lax.all_gather(log_total, 'blk', axis=0, tiled=True)  19.5 us
    dot_general x3, matrix products, contract_first(): lax.dot_general(left, right, (((0,), (0,)), ((), ())), preferred_element_...  18.9 us
    all_gather x1, blocking collectives, on_device(): lax.all_gather(own_ids, 'blk', axis=0, tiled=True)  18 us
    unnamed x13, local copies, waits for them, and re-layouts  9.76 us
    all_gather x1, waiting for transfers between devices, on_device(): shard_rows = lax.all_gather(query_vecs, 'blk', axis=0, tiled=True)  7.98 us
  transfers between devices with their start and end apart: 3, of which 2 were waited for; matrix products, arithmetic and copies ran while one was open for 8% of the time, Pallas kernels for 0%

commit v1 on v0

v1 whole, which is shorter than its diff:
```python
import functools
import math

import jax
import jax.numpy as jnp
from jax import lax
from jax.experimental import pallas as pl
from jax.experimental.pallas import tpu as pltpu
from jax.sharding import PartitionSpec as P

EXCLUDED = -1e30
LANES = 128
LOW = 4
F32 = jnp.float32
BF16 = jnp.bfloat16


def contract_last(left, right):
    return lax.dot_general(left, right, (((1,), (1,)), ((), ())), preferred_element_type=F32)


def matmul(left, right):
    return jnp.dot(left, right, preferred_element_type=F32)


def as_column(row):
    return jnp.transpose(jnp.broadcast_to(row, (LANES, row.shape[1])))


def as_wide_column(row, width):
    column = as_column(row)
    return jnp.concatenate([column] * (width // LANES), axis=1)


def kernel(
    high, parts,
    qx_ref, ix_ref, ids_ref, buckets_ref, logq_ref, qw_ref, iw_ref,
    grad_q_ref, grad_i_ref, loss_ref,
    q_all, i_all, meta_q, meta_i, i_turned, qx_turned, ix_turned,
    id_col, corr_col, score, weight, q_scaled,
    stats, o_send, o_recv, o_own, u_send, u_recv, u_own,
    grads, half_recv, acc, send1, recv1, acc1, send2, recv2, acc2, send3, recv3, full, loss_buf,
    sem_qs, sem_qr, sem_is, sem_ir, sem_ms, sem_mr, sem_ns, sem_nr,
    sem_ss, sem_sr, sem_os, sem_or, sem_us, sem_ur,
    sem_hs, sem_hr, sem_1s, sem_1r, sem_2s, sem_2r, sem_3s, sem_3r,
    sem_ls, sem_lr, sem_g3s, sem_g3r, sem_g2s, sem_g2r, sem_g1s, sem_g1r, sem_g0s, sem_g0r,
):
    rows, width = qx_ref.shape
    embed = qw_ref.shape[1]
    group_items = LOW * rows
    scaling = 1.0 / math.sqrt(embed)
    me = lax.axis_index("blk")
    part = lax.axis_index("dp")
    hi, lo = me // LOW, me % LOW
    mid, core = lo // 2, lo % 2

    def by_high(k):
        return {"blk": lax.rem(hi + k, high) * LOW + lo}

    def by_low(k):
        return {"blk": hi * LOW + lax.rem(lo + k, LOW)}

    def by_part(k):
        return {"dp": lax.rem(part + k, parts)}

    by_core = {"blk": hi * LOW + mid * 2 + (1 - core)}
    by_mid = {"blk": hi * LOW + (1 - mid) * 2 + core}

    def send(src, dst, send_sem, recv_sem, device):
        copy = pltpu.make_async_remote_copy(
            src_ref=src, dst_ref=dst, send_sem=send_sem, recv_sem=recv_sem,
            device_id=device, device_id_type=pl.DeviceIdType.MESH,
        )
        copy.start()
        return copy

    barrier = pltpu.get_barrier_semaphore()
    greeted = [by_high(k) for k in range(1, high)] + [by_low(k) for k in range(1, LOW)]
    greeted += [by_part(k) for k in range(1, parts)]
    for device in greeted:
        pl.semaphore_signal(barrier, inc=1, device_id=device, device_id_type=pl.DeviceIdType.MESH)

    q_all[0] = matmul(qx_ref[...], qw_ref[...]).astype(BF16)
    logq_col = as_column(logq_ref[...])
    count = logq_col.shape[0]
    pieces = []
    for c in range(rows // LANES):
        lane = slice(c * LANES, (c + 1) * LANES)
        bucket = lax.broadcasted_iota(jnp.int32, (count, LANES), 0)
        chosen = jnp.where(bucket == buckets_ref[:, lane], logq_col, 0.0)
        pieces.append(jnp.sum(chosen, axis=0, keepdims=True))
    meta_q[0, 0:1, :] = ids_ref[...].astype(F32)
    meta_q[0, 1:2, :] = jnp.concatenate(pieces, axis=1)
    meta_q[0, 2:8, :] = jnp.zeros((6, rows), F32)
    meta_i[0] = meta_q[0]
    pl.semaphore_wait(barrier, len(greeted))

    copies_q, copies_m, copies_i, copies_n = [], [], [], []
    for k in range(1, high):
        copies_q.append(send(q_all.at[0], q_all.at[k], sem_qs.at[k], sem_qr.at[k], by_high(k)))
        copies_m.append(send(meta_q.at[0], meta_q.at[k], sem_ms.at[k], sem_mr.at[k], by_high(k)))
    i_all[0] = matmul(ix_ref[...], iw_ref[...]).astype(BF16)
    for k in range(1, LOW):
        copies_n.append(send(meta_i.at[0], meta_i.at[k], sem_ns.at[k], sem_nr.at[k], by_low(k)))
        copies_i.append(send(i_all.at[0], i_all.at[k], sem_is.at[k], sem_ir.at[k], by_low(k)))

    qx_turned[...] = jnp.transpose(qx_ref[...])
    ix_turned[...] = jnp.transpose(ix_ref[...])

    for k in range(LOW):
        if k:
            copies_i[k - 1].wait_recv()
            copies_n[k - 1].wait_recv()
        span = slice(k * rows, (k + 1) * rows)
        i_turned[:, span] = jnp.transpose(i_all[k])
        id_col[span, :] = as_column(meta_i[k, 0:1, :])
        corr_col[span, :] = as_column(meta_i[k, 1:2, :])

    step_rows = 32
    lane_chunks = rows // LANES
    copies_o = []
    positive = None
    for k in range(high):
        if k:
            copies_q[k - 1].wait_recv()
            copies_m[k - 1].wait_recv()
        for j in range(LOW):
            score[j * rows:(j + 1) * rows, :] = contract_last(i_all[j], q_all[k])
        id_row = meta_q[k, 0:1, :]

        def mask_step(own, step, peak):
            start = pl.multiple_of(step * step_rows, step_rows)
            span = pl.ds(start, step_rows)
            new, diag = [], []
            for c in range(lane_chunks):
                lane = slice(c * LANES, (c + 1) * LANES)
                value = score[span, lane] * scaling - corr_col[span, :]
                same = id_col[span, :] == id_row[:, lane]
                if own:
                    row = lax.broadcasted_iota(jnp.int32, (step_rows, LANES), 0) + start
                    col = lax.broadcasted_iota(jnp.int32, (step_rows, LANES), 1) + c * LANES
                    on_diag = row == col
                    diag.append(jnp.sum(jnp.where(on_diag, value, 0.0).reshape(step_rows // 8, 8, LANES), axis=0))
                    same = same & jnp.logical_not(on_diag)
                value = jnp.where(same, EXCLUDED, value)
                score[span, lane] = value
                new.append(jnp.max(value.reshape(step_rows // 8, 8, LANES), axis=0))
            top = jnp.concatenate(new, axis=1)
            if own:
                return jnp.maximum(peak[0], top), peak[1] + jnp.concatenate(diag, axis=1)
            return jnp.maximum(peak, top)

        peak = jnp.full((8, rows), EXCLUDED, F32)
        total_steps = group_items // step_rows
        first = 0
        if k == 0:
            first = rows // step_rows
            peak, diag = lax.fori_loop(
                0, first, functools.partial(mask_step, True), (peak, jnp.zeros((8, rows), F32))
            )
            positive = jnp.sum(diag, axis=0, keepdims=True)
        peak = lax.fori_loop(first, total_steps, functools.partial(mask_step, False), peak)
        peak = jnp.max(peak, axis=0, keepdims=True)

        def exp_step(step, total):
            span = pl.ds(pl.multiple_of(step * step_rows, step_rows), step_rows)
            value = jnp.exp(score[span, :] - peak)
            weight[span, k * rows:(k + 1) * rows] = value.astype(BF16)
            return total + jnp.sum(value.reshape(step_rows // 8, 8, rows), axis=0)

        total = lax.fori_loop(0, total_steps, exp_step, jnp.zeros((8, rows), F32))
        stats[0, 2 * k:2 * k + 1, :] = peak
        stats[0, 2 * k + 1:2 * k + 2, :] = jnp.sum(total, axis=0, keepdims=True)
        partial = matmul(i_turned[...], weight[:, k * rows:(k + 1) * rows])
        if k == 0:
            o_own[...] = partial
        else:
            o_send[k] = partial.astype(BF16)
            copies_o.append(
                send(o_send.at[k], o_recv.at[k], sem_os.at[k], sem_or.at[k], by_high(high - k))
            )

    copies_s = [
        send(stats.at[0], stats.at[k], sem_ss.at[k], sem_sr.at[k], by_high(k)) for k in range(1, high)
    ]
    for copy in copies_s:
        copy.wait_recv()
    log_total = []
    for k in range(high):
        peaks = [stats[d, 2 * ((k - d) % high):2 * ((k - d) % high) + 1, :] for d in range(high)]
        sums = [stats[d, 2 * ((k - d) % high) + 1:2 * ((k - d) % high) + 2, :] for d in range(high)]
        top = functools.reduce(jnp.maximum, peaks)
        whole = functools.reduce(jnp.add, [s * jnp.exp(p - top) for p, s in zip(peaks, sums)])
        log_total.append(top + jnp.log(whole))
        factor = jnp.exp(peaks[0] - log_total[k])
        q_scaled[k * rows:(k + 1) * rows, :] = (
            q_all[k].astype(F32) * as_wide_column(factor, embed)
        ).astype(BF16)

    copies_u = []
    for j in list(range(1, LOW)) + [0]:
        sums = matmul(weight[j * rows:(j + 1) * rows, :], q_scaled[...])
        if j:
            u_send[j] = sums.astype(BF16)
            copies_u.append(
                send(u_send.at[j], u_recv.at[j], sem_us.at[j], sem_ur.at[j], by_low(LOW - j))
            )
        else:
            u_own[...] = sums

    own_total = o_own[...] * jnp.exp(stats[0, 0:1, :] - log_total[0])
    for k in range(1, high):
        copies_o[k - 1].wait_recv()
        d = high - k
        own_total += o_recv[k].astype(F32) * jnp.exp(stats[d, 2 * k:2 * k + 1, :] - log_total[0])
    query_grad = ((jnp.transpose(own_total) - i_all[0].astype(F32)) * scaling).astype(BF16)
    grads[0] = matmul(qx_turned[...], query_grad)
    lost = jnp.sum(log_total[0] - positive, axis=1, keepdims=True)

    sums = u_own[...]
    for j in range(1, LOW):
        copies_u[j - 1].wait_recv()
        sums += u_recv[j].astype(F32)
    item_grad = ((sums - q_all[0].astype(F32)) * scaling).astype(BF16)
    grads[1] = matmul(ix_turned[...], item_grad)

    pending = copies_q + copies_m + copies_i + copies_n + copies_o + copies_s + copies_u

    loss_buf[0] = jnp.broadcast_to(lost, (8, LANES))
    slot = 0

    def loss_round(partners):
        nonlocal slot
        base, copies = slot, []
        for n, device in enumerate(partners):
            at = base + 1 + n
            copies.append(send(loss_buf.at[base], loss_buf.at[at], sem_ls.at[at], sem_lr.at[at], device))
        return base, copies

    def loss_sum(base, copies):
        nonlocal slot
        value = loss_buf[base]
        for n, copy in enumerate(copies):
            copy.wait_recv()
            value += loss_buf[base + 1 + n]
        pending.extend(copies)
        slot = base + 1 + len(copies)
        loss_buf[slot] = value

    copy = send(grads.at[1 - core], half_recv, sem_hs.at[0], sem_hr.at[0], by_core)
    base, copies = loss_round([by_core])
    copy.wait_recv()
    acc[...] = grads[core].reshape(acc.shape) + half_recv[...].reshape(acc.shape)
    pending.append(copy)
    loss_sum(base, copies)

    moved = []
    for k in range(1, parts):
        send1[k] = acc[lax.rem(part + k, parts)].astype(BF16)
        moved.append(send(send1.at[k], recv1.at[k], sem_1s.at[k], sem_1r.at[k], by_part(k)))
    base, copies = loss_round([by_part(k) for k in range(1, parts)])
    value = acc[part]
    for k in range(1, parts):
        moved[k - 1].wait_recv()
        value += recv1[k].astype(F32)
    acc1[...] = value.reshape(acc1.shape)
    pending.extend(moved)
    loss_sum(base, copies)

    send2[...] = acc1[1 - mid].astype(BF16)
    copy = send(send2, recv2, sem_2s.at[0], sem_2r.at[0], by_mid)
    base, copies = loss_round([by_mid])
    copy.wait_recv()
    acc2[...] = (acc1[mid] + recv2[...].astype(F32)).reshape(acc2.shape)
    pending.append(copy)
    loss_sum(base, copies)

    moved = []
    for k in range(1, high):
        send3[k] = acc2[lax.rem(hi + k, high)].astype(BF16)
        moved.append(send(send3.at[k], recv3.at[k], sem_3s.at[k], sem_3r.at[k], by_high(k)))
    base, copies = loss_round([by_high(k) for k in range(1, high)])
    value = acc2[hi]
    for k in range(1, high):
        moved[k - 1].wait_recv()
        value += recv3[k].astype(F32)
    full[core, part, mid, hi] = value.astype(BF16)
    pending.extend(moved)
    loss_sum(base, copies)

    place = full.at[core, part, mid, hi]
    moved = [send(place, place, sem_g3s.at[k], sem_g3r.at[k], by_high(k)) for k in range(1, high)]
    for copy in moved:
        copy.wait_recv()
    pending.extend(moved)
    place = full.at[core, part, mid]
    copy = send(place, place, sem_g2s.at[0], sem_g2r.at[0], by_mid)
    copy.wait_recv()
    pending.append(copy)
    place = full.at[core, part]
    moved = [send(place, place, sem_g1s.at[k], sem_g1r.at[k], by_part(k)) for k in range(1, parts)]
    for copy in moved:
        copy.wait_recv()
    pending.extend(moved)
    place = full.at[core]
    copy = send(place, place, sem_g0s.at[0], sem_g0r.at[0], by_core)
    copy.wait_recv()
    pending.append(copy)

    piece = full.shape[4]
    at = 0
    for a in range(parts):
        for b in range(2):
            for c in range(high):
                grad_q_ref[at:at + piece, :] = full[0, a, b, c].astype(F32)
                grad_i_ref[at:at + piece, :] = full[1, a, b, c].astype(F32)
                at += piece
    loss_ref[...] = loss_buf[slot] * (1.0 / (parts * high * LOW * rows))
    for copy in pending:
        copy.wait_send()


def on_device(high, parts, query_feats, item_feats, item_ids, bucket_ids, bucket_logq, query_tower, item_tower):
    rows, width = query_feats.shape[1:]
    embed = query_tower.shape[1]
    items = LOW * rows
    stat_rows = -(-2 * high // 8) * 8
    rounds = 1 + 1 + 1 + (parts - 1) + 1 + 1 + 1 + (high - 1) + 1
    r1 = width // parts
    r2 = r1 // 2
    r3 = r2 // high
    vmem, dma = pltpu.VMEM, pltpu.SemaphoreType.DMA
    block = (rows, embed)
    scratch = [
        vmem((high,) + block, BF16), vmem((LOW,) + block, BF16),
        vmem((high, 8, rows), F32), vmem((LOW, 8, rows), F32),
        vmem((embed, items), BF16), vmem((width, rows), BF16), vmem((width, rows), BF16),
        vmem((items, LANES), F32), vmem((items, LANES), F32),
        vmem((items, rows), F32), vmem((items, high * rows), BF16), vmem((high * rows, embed), BF16),
        vmem((high, stat_rows, rows), F32),
        vmem((high, embed, rows), BF16), vmem((high, embed, rows), BF16), vmem((embed, rows), F32),
        vmem((LOW,) + block, BF16), vmem((LOW,) + block, BF16), vmem(block, F32),
        vmem((2, width, embed), F32), vmem((width, embed), F32), vmem((parts, r1, embed), F32),
        vmem((parts, r1, embed), BF16), vmem((parts, r1, embed), BF16), vmem((2, r2, embed), F32),
        vmem((r2, embed), BF16), vmem((r2, embed), BF16), vmem((high, r3, embed), F32),
        vmem((high, r3, embed), BF16), vmem((high, r3, embed), BF16),
        vmem((2, parts, 2, high, r3, embed), BF16), vmem((rounds, 8, LANES), F32),
    ]
    scratch += [dma((n,)) for n in (high, high, LOW, LOW, high, high, LOW, LOW)]
    scratch += [dma((n,)) for n in (high, high, high, high, LOW, LOW)]
    scratch += [dma((n,)) for n in (1, 1, parts, parts, 1, 1, high, high)]
    scratch += [dma((n,)) for n in (rounds, rounds, high, high, 1, 1, parts, parts, 1, 1)]
    grad_q, grad_i, loss = pl.pallas_call(
        functools.partial(kernel, high, parts),
        out_shape=(
            jax.ShapeDtypeStruct((width, embed), F32),
            jax.ShapeDtypeStruct((width, embed), F32),
            jax.ShapeDtypeStruct((8, LANES), F32),
        ),
        in_specs=[pl.BlockSpec(memory_space=pltpu.VMEM)] * 7,
        out_specs=[pl.BlockSpec(memory_space=pltpu.VMEM)] * 3,
        scratch_shapes=scratch,
        compiler_params=pltpu.CompilerParams(
            collective_id=0, has_side_effects=True, vmem_limit_bytes=60 * 1024 * 1024
        ),
        name="two_tower",
    )(
        query_feats[0], item_feats[0], item_ids, bucket_ids, bucket_logq[None, :], query_tower, item_tower
    )
    return grad_q, grad_i, loss[0, 0]


def solution(mesh):
    high = mesh.shape["blk"] // LOW
    return jax.shard_map(
        functools.partial(on_device, high, mesh.shape["dp"]),
        mesh=mesh,
        in_specs=(
            P("dp", "blk", None), P("dp", "blk", None), P("dp", "blk"), P("dp", "blk"), P(), P(), P(),
        ),
        out_specs=(P(), P(), P()),
        check_vma=False,
    )
```

time: 272 us -> 100 us (0.37)
  blocking collectives: 100 us -> 0 us
  waiting for transfers between devices: 100 us -> 0 us
  Pallas kernels: 0 us -> 94.8 us
  matrix products: 28.4 us -> 0 us
  between operations: 15.6 us -> 0.64 us
  other arithmetic: 11.7 us -> 0 us
  local copies, waits for them, and re-layouts: 13.3 us -> 4.52 us
    pallas_call x0 -> x1, Pallas kernels: none -> 94.8 us  [on_device(): pl.pallas_call(functools.partial(kernel, high, parts), out_shape=(jax.Sha...]
    psum x1 -> x0, waiting for transfers between devices: 92 us -> none  [on_device(): lax.psum((tower_query, tower_item, loss_local), ('blk', 'dp'))]
    all_gather x3 -> x0, blocking collectives: 60.8 us -> none  [the longest x1 23.3 us: on_device(): lax.all_gather(bucket_ids[0], 'blk', axis=0, tiled=True)]
    psum x1 -> x0, blocking collectives: 39.4 us -> none  [on_device(): lax.psum((tower_query, tower_item, loss_local), ('blk', 'dp'))]
    dot_general x6 -> x0, matrix products: 28.4 us -> none  [the longest x3 18.9 us: contract_first(): lax.dot_general(left, right, (((0,), (0,)), ((), ())), preferred_element_...]
    reduce_sum x3 -> x0, other arithmetic: 11 us -> none  [the longest x1 5.99 us: on_device(): jnp.sum(jnp.exp(masked - peaks[:, None]), axis=1)]
    all_gather x2 -> x0, waiting for transfers between devices: 7.98 us -> none  [the longest x1 7.98 us: on_device(): shard_rows = lax.all_gather(query_vecs, 'blk', axis=0, tiled=True)]
    unnamed x13 -> x4, local copies, waits for them, and re-layouts: 9.76 us -> 3.32 us
  transfers between devices with their start and end apart: 3 -> 0, of which waited for: 2 -> 0; matrix products, arithmetic and copies ran while one was open for 8% -> 0% of each run, Pallas kernels for 0% -> 0%
where the time goes in v1:
time: 100 us
  Pallas kernels  94.8 us (95%)
  local copies, waits for them, and re-layouts  4.52 us (5%)
    pallas_call x1, Pallas kernels, on_device(): pl.pallas_call(functools.partial(kernel, high, parts), out_shape=(jax.Sha...  94.8 us
    unnamed x4, local copies, waits for them, and re-layouts  3.32 us

profile of v1, /device:TPU:1, one launch (start us, length us, event | category | flops | bytes accessed | tf_op | source)
XLA Modules:
  0.0 100.0 jit_solution(9392355672399744434)
XLA Ops:
  0.6 94.8 %two_tower.1 = (f32[1024,256]{1,0:T(8,128)}, f32[1024,256]{1,0:T(8,128)}, f32[8,128]{1,0:T(8,128)}) custom-call(bf16[384,1024]{1,0:T(8,128)(2,1)} %bitcast.4, bf16[384,1024]{1,0:T(8,128)(2,1)} %bitcast.5, s32[1,384]{1,0:T(1,128)} %ids_ref.1, s32[1,384]{1,0:T(1,128)} %buckets_ref.1, f32[1,256]{1,0:T(1,128)} %bitcast.6, bf16[1024,256]{1,0:T(8,128)(2,1)} %qw_ref.1, ...), custom_call_target="tpu_custom_call" | custom-call | tf_op jit(solution)/shard_map/two_tower/pallas_call | solution.py:353
  95.4 1.2 %slice.3 = f32[1,1]{1,0:T(1,128)} slice(f32[8,128]{1,0:T(8,128)} %get-tuple-element.8), slice={[0:1], [0:1]} | slice | bytes 8 | tf_op jit(solution)/shard_map/slice | solution.py:370
  96.6 0.0 copy-start
  96.6 2.4 %copy.12 = f32[1024,256]{1,0:T(8,128)} copy(f32[1024,256]{1,0:T(8,128)} %get-tuple-element.12) | data formatting | bytes 2097152
  99.0 0.0 copy-done
  99.0 1.0 copy.13
Async XLA Ops:
  96.6 2.4 %copy-start = (f32[1024,256]{1,0:T(8,128)S(1)}, f32[1024,256]{1,0:T(8,128)}, u32[]{:S(2)}) copy-start(f32[1024,256]{1,0:T(8,128)} %get-tuple-element.13) | copy-start | bytes 3145732

commit v2 on v1

v2 whole, which is shorter than its diff:
```python
import functools
import math

import jax
import jax.numpy as jnp
from jax import lax
from jax.experimental import pallas as pl
from jax.experimental.pallas import tpu as pltpu
from jax.sharding import PartitionSpec as P

EXCLUDED = -1e30
LANES = 128
LOW = 4
F32 = jnp.float32
BF16 = jnp.bfloat16


def contract_last(left, right):
    return lax.dot_general(left, right, (((1,), (1,)), ((), ())), preferred_element_type=F32)


def matmul(left, right):
    return jnp.dot(left, right, preferred_element_type=F32)


def as_column(row):
    return jnp.transpose(jnp.broadcast_to(row, (LANES, row.shape[1])))


def as_wide_column(row, width):
    column = as_column(row)
    return jnp.concatenate([column] * (width // LANES), axis=1)


def kernel(
    high, parts,
    qx_hbm, ix_hbm, ids_ref, buckets_ref, logq_ref, qw_hbm, iw_hbm,
    grad_ref, loss_ref,
    qx_ref, ix_ref, qw_ref, iw_ref,
    q_all, i_all, meta_q, meta_i, i_turned, qx_turned, ix_turned,
    id_col, corr_col, score, weight, q_scaled,
    stats, o_send, o_recv, o_own, u_send, u_recv, u_own, u_far,
    grads, half_recv, acc, send1, recv1, acc1, send2, recv2, acc2, send3, recv3,
    sendb, recvb, accb, sendc, recvc, full, loss_buf,
    sem_in, sem_out,
    sem_qs, sem_qr, sem_is, sem_ir, sem_ms, sem_mr, sem_ns, sem_nr,
    sem_ss, sem_sr, sem_os, sem_or, sem_us, sem_ur,
    sem_hs, sem_hr, sem_1s, sem_1r, sem_2s, sem_2r, sem_3s, sem_3r,
    sem_bs, sem_br, sem_cs, sem_cr,
    sem_ls, sem_lr, sem_g3s, sem_g3r, sem_g2s, sem_g2r, sem_g1s, sem_g1r, sem_g0s, sem_g0r,
):
    rows, width = qx_ref.shape
    embed = qw_ref.shape[1]
    scaling = 1.0 / math.sqrt(embed)
    me = lax.axis_index("blk")
    part = lax.axis_index("dp")
    hi, lo = me // LOW, me % LOW
    mid, core = lo // 2, lo % 2

    def by_high(k):
        return {"blk": lax.rem(hi + k, high) * LOW + lo}

    def by_part(k):
        return {"dp": lax.rem(part + k, parts)}

    by_core = {"blk": hi * LOW + mid * 2 + (1 - core)}
    by_mid = {"blk": hi * LOW + (1 - mid) * 2 + core}

    def send(src, dst, send_sem, recv_sem, device):
        copy = pltpu.make_async_remote_copy(
            src_ref=src, dst_ref=dst, send_sem=send_sem, recv_sem=recv_sem,
            device_id=device, device_id_type=pl.DeviceIdType.MESH,
        )
        copy.start()
        return copy

    barrier = pltpu.get_barrier_semaphore()
    greeted = [by_high(k) for k in range(1, high)] + [by_core, by_mid]
    greeted += [by_part(k) for k in range(1, parts)]
    for device in greeted:
        pl.semaphore_signal(barrier, inc=1, device_id=device, device_id_type=pl.DeviceIdType.MESH)

    loads = [
        pltpu.make_async_copy(src, dst, sem_in.at[n])
        for n, (src, dst) in enumerate(
            [(qw_hbm, qw_ref), (qx_hbm, qx_ref), (iw_hbm, iw_ref), (ix_hbm, ix_ref)]
        )
    ]
    for load in loads:
        load.start()

    logq_col = as_column(logq_ref[...])
    count = logq_col.shape[0]
    pieces = []
    for c in range(rows // LANES):
        lane = slice(c * LANES, (c + 1) * LANES)
        bucket = lax.broadcasted_iota(jnp.int32, (count, LANES), 0)
        chosen = jnp.where(bucket == buckets_ref[:, lane], logq_col, 0.0)
        pieces.append(jnp.sum(chosen, axis=0, keepdims=True))
    meta_q[0, 0:1, :] = ids_ref[...].astype(F32)
    meta_q[0, 1:2, :] = jnp.concatenate(pieces, axis=1)
    meta_q[0, 2:8, :] = jnp.zeros((6, rows), F32)
    meta_i[0] = meta_q[0]
    loads[0].wait()
    loads[1].wait()
    q_all[0] = matmul(qx_ref[...], qw_ref[...]).astype(BF16)
    pl.semaphore_wait(barrier, len(greeted))

    copies_q, copies_m, copies_i, copies_n = [], [], [], []
    for k in range(1, high):
        copies_q.append(send(q_all.at[0], q_all.at[k], sem_qs.at[k], sem_qr.at[k], by_high(k)))
        copies_m.append(send(meta_q.at[0], meta_q.at[k], sem_ms.at[k], sem_mr.at[k], by_high(k)))
    loads[2].wait()
    loads[3].wait()
    i_all[0] = matmul(ix_ref[...], iw_ref[...]).astype(BF16)
    near = [None, by_core, by_mid, by_core]
    copies_n = [None] * LOW
    copies_i = [None] * LOW

    def spread(source, slot):
        copies_n[slot] = send(
            meta_i.at[source], meta_i.at[slot], sem_ns.at[slot], sem_nr.at[slot], near[slot]
        )
        copies_i[slot] = send(
            i_all.at[source], i_all.at[slot], sem_is.at[slot], sem_ir.at[slot], near[slot]
        )

    spread(0, 2)
    spread(0, 1)

    qx_turned[...] = jnp.transpose(qx_ref[...])
    ix_turned[...] = jnp.transpose(ix_ref[...])

    def prepare(j):
        span = slice(j * rows, (j + 1) * rows)
        i_turned[:, span] = jnp.transpose(i_all[j])
        id_col[span, :] = as_column(meta_i[j, 0:1, :])
        corr_col[span, :] = as_column(meta_i[j, 1:2, :])

    prepare(0)
    lane_chunks = rows // LANES
    copies_o = []
    positive = None
    for k in range(high):
        if k:
            copies_q[k - 1].wait_recv()
            copies_m[k - 1].wait_recv()
        id_row = meta_q[k, 0:1, :]
        peaks = [jnp.full((8, LANES), EXCLUDED, F32)] * lane_chunks
        for j in range(LOW):
            if k == 0 and j:
                copies_i[j].wait_recv()
                copies_n[j].wait_recv()
                if j == 2:
                    spread(2, 3)
                prepare(j)
            span = slice(j * rows, (j + 1) * rows)
            raw = contract_last(i_all[j], q_all[k])
            if k == 0 and j == 0:
                row = lax.broadcasted_iota(jnp.int32, (rows, LANES), 0)
                col = lax.broadcasted_iota(jnp.int32, (rows, LANES), 1)
                diag = []
            for c in range(lane_chunks):
                lane = slice(c * LANES, (c + 1) * LANES)
                value = raw[:, lane] * scaling - corr_col[span, :]
                same = id_col[span, :] == id_row[:, lane]
                if k == 0 and j == 0:
                    on_diag = row == col + c * LANES
                    diag.append(jnp.sum(jnp.where(on_diag, value, 0.0), axis=0, keepdims=True))
                    same = same & jnp.logical_not(on_diag)
                value = jnp.where(same, EXCLUDED, value)
                score[span, lane] = value
                peaks[c] = jnp.maximum(peaks[c], jnp.max(value.reshape(rows // 8, 8, LANES), axis=0))
            if k == 0 and j == 0:
                positive = jnp.concatenate(diag, axis=1)
        peak = jnp.max(jnp.concatenate(peaks, axis=1), axis=0, keepdims=True)
        total = jnp.zeros((8, rows), F32)
        for j in range(LOW):
            span = slice(j * rows, (j + 1) * rows)
            value = jnp.exp(score[span, :] - peak)
            weight[span, k * rows:(k + 1) * rows] = value.astype(BF16)
            total += jnp.sum(value.reshape(rows // 8, 8, rows), axis=0)
        stats[0, 2 * k:2 * k + 1, :] = peak
        stats[0, 2 * k + 1:2 * k + 2, :] = jnp.sum(total, axis=0, keepdims=True)
        partial = matmul(i_turned[...], weight[:, k * rows:(k + 1) * rows])
        if k == 0:
            o_own[...] = partial
        else:
            o_send[k] = partial.astype(BF16)
            copies_o.append(
                send(o_send.at[k], o_recv.at[k], sem_os.at[k], sem_or.at[k], by_high(high - k))
            )

    copies_s = [
        send(stats.at[0], stats.at[k], sem_ss.at[k], sem_sr.at[k], by_high(k)) for k in range(1, high)
    ]
    for copy in copies_s:
        copy.wait_recv()
    log_total = []
    for k in range(high):
        peaks = [stats[d, 2 * ((k - d) % high):2 * ((k - d) % high) + 1, :] for d in range(high)]
        sums = [stats[d, 2 * ((k - d) % high) + 1:2 * ((k - d) % high) + 2, :] for d in range(high)]
        top = functools.reduce(jnp.maximum, peaks)
        whole = functools.reduce(jnp.add, [s * jnp.exp(p - top) for p, s in zip(peaks, sums)])
        log_total.append(top + jnp.log(whole))
        factor = jnp.exp(peaks[0] - log_total[k])
        q_scaled[k * rows:(k + 1) * rows, :] = (
            q_all[k].astype(F32) * as_wide_column(factor, embed)
        ).astype(BF16)

    def item_sums(j):
        return matmul(weight[j * rows:(j + 1) * rows, :], q_scaled[...])

    copies_u = [None] * LOW
    for j in (3, 1):
        u_send[j] = item_sums(j).astype(BF16)
        copies_u[j] = send(u_send.at[j], u_recv.at[j], sem_us.at[j], sem_ur.at[j], by_core)
    u_far[...] = item_sums(2)
    copies_u[3].wait_recv()
    u_send[2] = (u_far[...] + u_recv[3].astype(F32)).astype(BF16)
    copies_u[2] = send(u_send.at[2], u_recv.at[2], sem_us.at[2], sem_ur.at[2], by_mid)
    u_own[...] = item_sums(0)

    own_total = o_own[...] * jnp.exp(stats[0, 0:1, :] - log_total[0])
    for k in range(1, high):
        copies_o[k - 1].wait_recv()
        d = high - k
        own_total += o_recv[k].astype(F32) * jnp.exp(stats[d, 2 * k:2 * k + 1, :] - log_total[0])
    query_grad = ((jnp.transpose(own_total) - i_all[0].astype(F32)) * scaling).astype(BF16)
    grads[0] = matmul(qx_turned[...], query_grad)
    lost = jnp.sum(log_total[0] - positive, axis=1, keepdims=True)

    sums = u_own[...]
    for j in (1, 2):
        copies_u[j].wait_recv()
        sums += u_recv[j].astype(F32)
    item_grad = ((sums - q_all[0].astype(F32)) * scaling).astype(BF16)
    grads[1] = matmul(ix_turned[...], item_grad)

    pending = copies_q + copies_m + copies_i[1:] + copies_n[1:] + copies_o + copies_s + copies_u[1:]

    loss_buf[0] = jnp.broadcast_to(lost, (8, LANES))
    slot = 0

    def loss_round(partners):
        nonlocal slot
        base, copies = slot, []
        for n, device in enumerate(partners):
            at = base + 1 + n
            copies.append(send(loss_buf.at[base], loss_buf.at[at], sem_ls.at[at], sem_lr.at[at], device))
        return base, copies

    def loss_sum(base, copies):
        nonlocal slot
        value = loss_buf[base]
        for n, copy in enumerate(copies):
            copy.wait_recv()
            value += loss_buf[base + 1 + n]
        pending.extend(copies)
        slot = base + 1 + len(copies)
        loss_buf[slot] = value

    copy = send(grads.at[1 - core], half_recv, sem_hs.at[0], sem_hr.at[0], by_core)
    base, copies = loss_round([by_core])
    copy.wait_recv()
    acc[...] = (grads[core] + half_recv[...]).reshape(acc.shape)
    pending.append(copy)
    loss_sum(base, copies)
    base, copies = loss_round([by_part(k) for k in range(1, parts)])

    @pl.when(core == 0)
    def _():
        moved = []
        for k in range(1, parts):
            send1[k] = acc[lax.rem(part + k, parts)].astype(BF16)
            moved.append(send(send1.at[k], recv1.at[k], sem_1s.at[k], sem_1r.at[k], by_part(k)))
        value = acc[part]
        for k in range(1, parts):
            moved[k - 1].wait_recv()
            value += recv1[k].astype(F32)
        acc1[...] = value
        send2[...] = acc1[1 - mid].astype(BF16)
        moved.append(send(send2, recv2, sem_2s.at[0], sem_2r.at[0], by_mid))
        moved[-1].wait_recv()
        acc2[...] = acc1[mid] + recv2[...].astype(F32)
        for copy in moved:
            copy.wait_send()

    @pl.when(core == 1)
    def _():
        for k in range(parts):
            sendb[k] = acc[k, 1 - mid].astype(BF16)
        moved = [send(sendb, recvb, sem_bs.at[0], sem_br.at[0], by_mid)]
        moved[0].wait_recv()
        for k in range(parts):
            accb[k] = acc[k, mid] + recvb[k].astype(F32)
        for k in range(1, parts):
            sendc[k] = accb[lax.rem(part + k, parts)].astype(BF16)
            moved.append(send(sendc.at[k], recvc.at[k], sem_cs.at[k], sem_cr.at[k], by_part(k)))
        value = accb[part]
        for k in range(1, parts):
            moved[k].wait_recv()
            value += recvc[k].astype(F32)
        acc2[...] = value
        for copy in moved:
            copy.wait_send()

    loss_sum(base, copies)
    base, copies = loss_round([by_mid])
    moved = []
    for k in range(1, high):
        send3[k] = acc2[lax.rem(hi + k, high)].astype(BF16)
        moved.append(send(send3.at[k], recv3.at[k], sem_3s.at[k], sem_3r.at[k], by_high(k)))
    value = acc2[hi]
    for k in range(1, high):
        moved[k - 1].wait_recv()
        value += recv3[k].astype(F32)
    full[core, part, mid, hi] = value.astype(BF16)
    pending.extend(moved)
    loss_sum(base, copies)

    place = full.at[core, part, mid, hi]
    moved = [send(place, place, sem_g3s.at[k], sem_g3r.at[k], by_high(k)) for k in range(1, high)]
    base, copies = loss_round([by_high(k) for k in range(1, high)])
    for copy in moved:
        copy.wait_recv()
    pending.extend(moved)

    @pl.when(core == 0)
    def _():
        place = full.at[core, part, mid]
        moved = [send(place, place, sem_g2s.at[0], sem_g2r.at[0], by_mid)]
        moved[0].wait_recv()
        place = full.at[core, part]
        for k in range(1, parts):
            moved.append(send(place, place, sem_g1s.at[k], sem_g1r.at[k], by_part(k)))
        for copy in moved[1:]:
            copy.wait_recv()
        for copy in moved:
            copy.wait_send()

    @pl.when(core == 1)
    def _():
        place = full.at[core, part, mid]
        first = [send(place, place, sem_g1s.at[k], sem_g1r.at[k], by_part(k)) for k in range(1, parts)]
        for copy in first:
            copy.wait_recv()
        second = []
        for k in range(parts):
            place = full.at[core, k, mid]
            second.append(send(place, place, sem_g2s.at[k], sem_g2r.at[k], by_mid))
        for copy in second:
            copy.wait_recv()
        for copy in first + second:
            copy.wait_send()

    place = full.at[core]
    copy = send(place, place, sem_g0s.at[0], sem_g0r.at[0], by_core)
    own_out = pltpu.make_async_copy(place, grad_ref.at[core], sem_out.at[0])
    own_out.start()
    loss_sum(base, copies)
    loss_ref[...] = loss_buf[slot, 0:1, 0:1] * (1.0 / (parts * high * LOW * rows))
    copy.wait_recv()
    pending.append(copy)
    other_out = pltpu.make_async_copy(full.at[1 - core], grad_ref.at[1 - core], sem_out.at[1])
    other_out.start()
    for copy in pending:
        copy.wait_send()
    own_out.wait()
    other_out.wait()


def on_device(high, parts, query_feats, item_feats, item_ids, bucket_ids, bucket_logq, query_tower, item_tower):
    rows, width = query_feats.shape[1:]
    embed = query_tower.shape[1]
    items = LOW * rows
    stat_rows = -(-2 * high // 8) * 8
    rounds = 1 + 1 + 1 + (parts - 1) + 1 + 1 + 1 + (high - 1) + 1
    r3 = width // (2 * parts * high)
    vmem, dma = pltpu.VMEM, pltpu.SemaphoreType.DMA
    block = (rows, embed)
    far = (2, high, r3, embed)
    wide = (parts, high, r3, embed)
    scratch = [
        vmem((rows, width), BF16), vmem((rows, width), BF16),
        vmem((width, embed), BF16), vmem((width, embed), BF16),
        vmem((high,) + block, BF16), vmem((LOW,) + block, BF16),
        vmem((high, 8, rows), F32), vmem((LOW, 8, rows), F32),
        vmem((embed, items), BF16), vmem((width, rows), BF16), vmem((width, rows), BF16),
        vmem((items, LANES), F32), vmem((items, LANES), F32),
        vmem((items, rows), F32), vmem((items, high * rows), BF16), vmem((high * rows, embed), BF16),
        vmem((high, stat_rows, rows), F32),
        vmem((high, embed, rows), BF16), vmem((high, embed, rows), BF16), vmem((embed, rows), F32),
        vmem((LOW,) + block, BF16), vmem((LOW,) + block, BF16), vmem(block, F32), vmem(block, F32),
        vmem((2, width, embed), F32), vmem((width, embed), F32), vmem((parts,) + far, F32),
        vmem((parts,) + far, BF16), vmem((parts,) + far, BF16), vmem(far, F32),
        vmem(far[1:], BF16), vmem(far[1:], BF16), vmem(far[1:], F32),
        vmem((high, r3, embed), BF16), vmem((high, r3, embed), BF16),
        vmem(wide, BF16), vmem(wide, BF16), vmem(wide, F32), vmem(wide, BF16), vmem(wide, BF16),
        vmem((2, parts) + far, BF16), vmem((rounds, 8, LANES), F32),
    ]
    scratch += [dma((n,)) for n in (4, 2)]
    scratch += [dma((n,)) for n in (high, high, LOW, LOW, high, high, LOW, LOW)]
    scratch += [dma((n,)) for n in (high, high, high, high, LOW, LOW)]
    scratch += [dma((n,)) for n in (1, 1, parts, parts, 1, 1, high, high)]
    scratch += [dma((n,)) for n in (1, 1, parts, parts)]
    scratch += [dma((n,)) for n in (rounds, rounds, high, high, parts, parts, parts, parts, 1, 1)]
    space = pltpu.VMEM
    grad, loss = pl.pallas_call(
        functools.partial(kernel, high, parts),
        out_shape=(
            jax.ShapeDtypeStruct((2, parts) + far, BF16),
            jax.ShapeDtypeStruct((1, 1), F32),
        ),
        in_specs=[
            pl.BlockSpec(memory_space=space)
            for space in (pl.ANY, pl.ANY, space, space, space, pl.ANY, pl.ANY)
        ],
        out_specs=(pl.BlockSpec(memory_space=pl.ANY), pl.BlockSpec(memory_space=space)),
        scratch_shapes=scratch,
        compiler_params=pltpu.CompilerParams(
            collective_id=0, has_side_effects=True, vmem_limit_bytes=60 * 1024 * 1024
        ),
        name="two_tower",
    )(
        query_feats[0], item_feats[0], item_ids, bucket_ids, bucket_logq[None, :], query_tower, item_tower
    )
    grad = grad.reshape(2, width, embed).astype(F32)
    return grad[0], grad[1], loss.reshape(())


def solution(mesh):
    high = mesh.shape["blk"] // LOW
    return jax.shard_map(
        functools.partial(on_device, high, mesh.shape["dp"]),
        mesh=mesh,
        in_specs=(
            P("dp", "blk", None), P("dp", "blk", None), P("dp", "blk"), P("dp", "blk"), P(), P(), P(),
        ),
        out_specs=(P(), P(), P()),
        check_vma=False,
    )
```

time: 100 us -> 97.4 us (0.974)
  Pallas kernels: 94.8 us -> 92 us
  between operations: 0.64 us -> 2.4 us
  local copies, waits for them, and re-layouts: 4.52 us -> 2.78 us
    unnamed x4 -> x0, local copies, waits for them, and re-layouts: 3.32 us -> none
    pallas_call x1, Pallas kernels: 94.8 us -> 92 us  [on_device(): pl.pallas_call(functools.partial(kernel, high, parts), out_shape=(jax.Sha...]
    slice x1, local copies, waits for them, and re-layouts: 1.19 us -> 2.78 us  [on_device(): return (grad[0], grad[1], loss.reshape(()))]
where the time goes in v2:
time: 97.4 us; the launch traced here: 97.2 us
  Pallas kernels  92 us (94%)
  local copies, waits for them, and re-layouts  2.78 us (3%)
  between operations  2.4 us (2%)
    pallas_call x1, Pallas kernels, on_device(): pl.pallas_call(functools.partial(kernel, high, parts), out_shape=(jax.Sha...  92 us
    slice x1, local copies, waits for them, and re-layouts, on_device(): return (grad[0], grad[1], loss.reshape(()))  2.78 us

profile of v2, /device:TPU:1, one launch (start us, length us, event | category | flops | bytes accessed | tf_op | source)
XLA Modules:
  0.0 97.2 jit_solution(3770481377870837758)
XLA Ops:
  0.6 92.0 %two_tower.1 = (bf16[2,2,2,4,64,256]{5,4,3,2,1,0:T(8,128)(2,1)}, f32[1,1]{1,0:T(1,128)}) custom-call(bf16[384,1024]{1,0:T(8,128)(2,1)} %bitcast.8, bf16[384,1024]{1,0:T(8,128)(2,1)} %bitcast.9, s32[1,384]{1,0:T(1,128)} %ids_ref.1, s32[1,384]{1,0:T(1,128)} %buckets_ref.1, f32[1,256]{1,0:T(1,128)} %bitcast.10, bf16[1024,256]{1,0:T(8,128)(2,1)} %qw_hbm.1, ...), custom_call_target="tpu_custom_call" | custom-call | tf_op jit(solution)/shard_map/two_tower/pallas_call | solution.py:409
  92.6 2.8 %fusion = (f32[1,2,2,4,64,256]{5,4,3,2,1,0:T(8,128)}, f32[1,2,2,4,64,256]{5,4,3,2,1,0:T(8,128)}) fusion(bf16[2,2,2,4,64,256]{5,4,3,2,1,0:T(8,128)(2,1)} %get-tuple-element.5), kind=kLoop, calls=%fused_computation | loop fusion | bytes 4194304 | tf_op jit(solution)/shard_map/slice | solution.py:429

commit v3 on v2

--- a/solution.py
+++ b/solution.py
@@ -40,12 +40,12 @@
     q_all, i_all, meta_q, meta_i, i_turned, qx_turned, ix_turned,
     id_col, corr_col, score, weight, q_scaled,
     stats, o_send, o_recv, o_own, u_send, u_recv, u_own, u_far,
-    grads, half_recv, acc, send1, recv1, acc1, send2, recv2, acc2, send3, recv3,
+    grads, half_recv, acc, acc2, send3, recv3,
     sendb, recvb, accb, sendc, recvc, full, loss_buf,
     sem_in, sem_out,
     sem_qs, sem_qr, sem_is, sem_ir, sem_ms, sem_mr, sem_ns, sem_nr,
     sem_ss, sem_sr, sem_os, sem_or, sem_us, sem_ur,
-    sem_hs, sem_hr, sem_1s, sem_1r, sem_2s, sem_2r, sem_3s, sem_3r,
+    sem_hs, sem_hr, sem_3s, sem_3r,
     sem_bs, sem_br, sem_cs, sem_cr,
     sem_ls, sem_lr, sem_g3s, sem_g3r, sem_g2s, sem_g2r, sem_g1s, sem_g1r, sem_g0s, sem_g0r,
 ):
@@ -187,13 +187,14 @@
             o_own[...] = partial
         else:
             o_send[k] = partial.astype(BF16)
-            copies_o.append(
-                send(o_send.at[k], o_recv.at[k], sem_os.at[k], sem_or.at[k], by_high(high - k))
-            )
 
     copies_s = [
         send(stats.at[0], stats.at[k], sem_ss.at[k], sem_sr.at[k], by_high(k)) for k in range(1, high)
     ]
+    for k in range(1, high):
+        copies_o.append(
+            send(o_send.at[k], o_recv.at[k], sem_os.at[k], sem_or.at[k], by_high(high - k))
+        )
     for copy in copies_s:
         copy.wait_recv()
     log_total = []
@@ -221,6 +222,13 @@
     copies_u[2] = send(u_send.at[2], u_recv.at[2], sem_us.at[2], sem_ur.at[2], by_mid)
     u_own[...] = item_sums(0)
 
+    sums = u_own[...]
+    for j in (1, 2):
+        copies_u[j].wait_recv()
+        sums += u_recv[j].astype(F32)
+    item_grad = ((sums - q_all[0].astype(F32)) * scaling).astype(BF16)
+    grads[1] = matmul(ix_turned[...], item_grad)
+
     own_total = o_own[...] * jnp.exp(stats[0, 0:1, :] - log_total[0])
     for k in range(1, high):
         copies_o[k - 1].wait_recv()
@@ -229,13 +237,6 @@
     query_grad = ((jnp.transpose(own_total) - i_all[0].astype(F32)) * scaling).astype(BF16)
     grads[0] = matmul(qx_turned[...], query_grad)
     lost = jnp.sum(log_total[0] - positive, axis=1, keepdims=True)
-
-    sums = u_own[...]
-    for j in (1, 2):
-        copies_u[j].wait_recv()
-        sums += u_recv[j].astype(F32)
-    item_grad = ((sums - q_all[0].astype(F32)) * scaling).astype(BF16)
-    grads[1] = matmul(ix_turned[...], item_grad)
 
     pending = copies_q + copies_m + copies_i[1:] + copies_n[1:] + copies_o + copies_s + copies_u[1:]
 
@@ -266,47 +267,27 @@
     acc[...] = (grads[core] + half_recv[...]).reshape(acc.shape)
     pending.append(copy)
     loss_sum(base, copies)
+    base, copies = loss_round([by_mid])
+    for k in range(parts):
+        sendb[k] = acc[k, 1 - mid].astype(BF16)
+    copy = send(sendb, recvb, sem_bs.at[0], sem_br.at[0], by_mid)
+    copy.wait_recv()
+    pending.append(copy)
+    for k in range(parts):
+        accb[k] = acc[k, mid] + recvb[k].astype(F32)
+    loss_sum(base, copies)
     base, copies = loss_round([by_part(k) for k in range(1, parts)])
-
-    @pl.when(core == 0)
-    def _():
-        moved = []
-        for k in range(1, parts):
-            send1[k] = acc[lax.rem(part + k, parts)].astype(BF16)
-            moved.append(send(send1.at[k], recv1.at[k], sem_1s.at[k], sem_1r.at[k], by_part(k)))
-        value = acc[part]
-        for k in range(1, parts):
-            moved[k - 1].wait_recv()
-            value += recv1[k].astype(F32)
-        acc1[...] = value
-        send2[...] = acc1[1 - mid].astype(BF16)
-        moved.append(send(send2, recv2, sem_2s.at[0], sem_2r.at[0], by_mid))
-        moved[-1].wait_recv()
-        acc2[...] = acc1[mid] + recv2[...].astype(F32)
-        for copy in moved:
-            copy.wait_send()
-
-    @pl.when(core == 1)
-    def _():
-        for k in range(parts):
-            sendb[k] = acc[k, 1 - mid].astype(BF16)
-        moved = [send(sendb, recvb, sem_bs.at[0], sem_br.at[0], by_mid)]
-        moved[0].wait_recv()
-        for k in range(parts):
-            accb[k] = acc[k, mid] + recvb[k].astype(F32)
-        for k in range(1, parts):
-            sendc[k] = accb[lax.rem(part + k, parts)].astype(BF16)
-            moved.append(send(sendc.at[k], recvc.at[k], sem_cs.at[k], sem_cr.at[k], by_part(k)))
-        value = accb[part]
-        for k in range(1, parts):
-            moved[k].wait_recv()
-            value += recvc[k].astype(F32)
-        acc2[...] = value
-        for copy in moved:
-            copy.wait_send()
-
-    loss_sum(base, copies)
-    base, copies = loss_round([by_mid])
+    moved = []
+    for k in range(1, parts):
+        sendc[k] = accb[lax.rem(part + k, parts)].astype(BF16)
+        moved.append(send(sendc.at[k], recvc.at[k], sem_cs.at[k], sem_cr.at[k], by_part(k)))
+    value = accb[part]
+    for k in range(1, parts):
+        moved[k - 1].wait_recv()
+        value += recvc[k].astype(F32)
+    acc2[...] = value
+    pending.extend(moved)
+
     moved = []
     for k in range(1, high):
         send3[k] = acc2[lax.rem(hi + k, high)].astype(BF16)
@@ -326,34 +307,18 @@
         copy.wait_recv()
     pending.extend(moved)
 
-    @pl.when(core == 0)
-    def _():
-        place = full.at[core, part, mid]
-        moved = [send(place, place, sem_g2s.at[0], sem_g2r.at[0], by_mid)]
-        moved[0].wait_recv()
-        place = full.at[core, part]
-        for k in range(1, parts):
-            moved.append(send(place, place, sem_g1s.at[k], sem_g1r.at[k], by_part(k)))
-        for copy in moved[1:]:
-            copy.wait_recv()
-        for copy in moved:
-            copy.wait_send()
-
-    @pl.when(core == 1)
-    def _():
-        place = full.at[core, part, mid]
-        first = [send(place, place, sem_g1s.at[k], sem_g1r.at[k], by_part(k)) for k in range(1, parts)]
-        for copy in first:
-            copy.wait_recv()
-        second = []
-        for k in range(parts):
-            place = full.at[core, k, mid]
-            second.append(send(place, place, sem_g2s.at[k], sem_g2r.at[k], by_mid))
-        for copy in second:
-            copy.wait_recv()
-        for copy in first + second:
-            copy.wait_send()
-
+    place = full.at[core, part, mid]
+    moved = [send(place, place, sem_g1s.at[k], sem_g1r.at[k], by_part(k)) for k in range(1, parts)]
+    for copy in moved:
+        copy.wait_recv()
+    pending.extend(moved)
+    moved = []
+    for k in range(parts):
+        place = full.at[core, k, mid]
+        moved.append(send(place, place, sem_g2s.at[k], sem_g2r.at[k], by_mid))
+    for copy in moved:
+        copy.wait_recv()
+    pending.extend(moved)
     place = full.at[core]
     copy = send(place, place, sem_g0s.at[0], sem_g0r.at[0], by_core)
     own_out = pltpu.make_async_copy(place, grad_ref.at[core], sem_out.at[0])
@@ -393,8 +358,7 @@
         vmem((high, embed, rows), BF16), vmem((high, embed, rows), BF16), vmem((embed, rows), F32),
         vmem((LOW,) + block, BF16), vmem((LOW,) + block, BF16), vmem(block, F32), vmem(block, F32),
         vmem((2, width, embed), F32), vmem((width, embed), F32), vmem((parts,) + far, F32),
-        vmem((parts,) + far, BF16), vmem((parts,) + far, BF16), vmem(far, F32),
-        vmem(far[1:], BF16), vmem(far[1:], BF16), vmem(far[1:], F32),
+        vmem(far[1:], F32),
         vmem((high, r3, embed), BF16), vmem((high, r3, embed), BF16),
         vmem(wide, BF16), vmem(wide, BF16), vmem(wide, F32), vmem(wide, BF16), vmem(wide, BF16),
         vmem((2, parts) + far, BF16), vmem((rounds, 8, LANES), F32),
@@ -402,7 +366,7 @@
     scratch += [dma((n,)) for n in (4, 2)]
     scratch += [dma((n,)) for n in (high, high, LOW, LOW, high, high, LOW, LOW)]
     scratch += [dma((n,)) for n in (high, high, high, high, LOW, LOW)]
-    scratch += [dma((n,)) for n in (1, 1, parts, parts, 1, 1, high, high)]
+    scratch += [dma((n,)) for n in (1, 1, high, high)]
     scratch += [dma((n,)) for n in (1, 1, parts, parts)]
     scratch += [dma((n,)) for n in (rounds, rounds, high, high, parts, parts, parts, parts, 1, 1)]
     space = pltpu.VMEM

time: 97.4 us -> 85.8 us (0.88)
  Pallas kernels: 92 us -> 80.4 us
    pallas_call x1, Pallas kernels: 92 us -> 80.4 us  [on_device(): pl.pallas_call(functools.partial(kernel, high, parts), out_shape=(jax.Sha...]
where the time goes in v3:
time: 85.8 us; the launch traced here: 85.6 us
  Pallas kernels  80.4 us (94%)
  local copies, waits for them, and re-layouts  2.78 us (3%)
  between operations  2.4 us (3%)
    pallas_call x1, Pallas kernels, on_device(): pl.pallas_call(functools.partial(kernel, high, parts), out_shape=(jax.Sha...  80.4 us
    slice x1, local copies, waits for them, and re-layouts, on_device(): return (grad[0], grad[1], loss.reshape(()))  2.78 us

profile of v3, /device:TPU:1, one launch (start us, length us, event | category | flops | bytes accessed | tf_op | source)
XLA Modules:
  0.0 85.6 jit_solution(17203483105361244835)
XLA Ops:
  0.6 80.4 %two_tower.1 = (bf16[2,2,2,4,64,256]{5,4,3,2,1,0:T(8,128)(2,1)}, f32[1,1]{1,0:T(1,128)}) custom-call(bf16[384,1024]{1,0:T(8,128)(2,1)} %bitcast.8, bf16[384,1024]{1,0:T(8,128)(2,1)} %bitcast.9, s32[1,384]{1,0:T(1,128)} %ids_ref.1, s32[1,384]{1,0:T(1,128)} %buckets_ref.1, f32[1,256]{1,0:T(1,128)} %bitcast.10, bf16[1024,256]{1,0:T(8,128)(2,1)} %qw_hbm.1, ...), custom_call_target="tpu_custom_call" | custom-call | tf_op jit(solution)/shard_map/two_tower/pallas_call | solution.py:373
  81.1 2.8 %fusion = (f32[1,2,2,4,64,256]{5,4,3,2,1,0:T(8,128)}, f32[1,2,2,4,64,256]{5,4,3,2,1,0:T(8,128)}) fusion(bf16[2,2,2,4,64,256]{5,4,3,2,1,0:T(8,128)(2,1)} %get-tuple-element.5), kind=kLoop, calls=%fused_computation | loop fusion | bytes 4194304 | tf_op jit(solution)/shard_map/slice | solution.py:393

commit v4 on v3

--- a/solution.py
+++ b/solution.py
@@ -40,13 +40,12 @@
     q_all, i_all, meta_q, meta_i, i_turned, qx_turned, ix_turned,
     id_col, corr_col, score, weight, q_scaled,
     stats, o_send, o_recv, o_own, u_send, u_recv, u_own, u_far,
-    grads, half_recv, acc, acc2, send3, recv3,
-    sendb, recvb, accb, sendc, recvc, full, loss_buf,
+    grads, half_recv, acc, send1, recv1, acc1, send2, recv2, acc2, send3, recv3,
+    full, loss_buf,
     sem_in, sem_out,
     sem_qs, sem_qr, sem_is, sem_ir, sem_ms, sem_mr, sem_ns, sem_nr,
     sem_ss, sem_sr, sem_os, sem_or, sem_us, sem_ur,
-    sem_hs, sem_hr, sem_3s, sem_3r,
-    sem_bs, sem_br, sem_cs, sem_cr,
+    sem_hs, sem_hr, sem_1s, sem_1r, sem_2s, sem_2r, sem_3s, sem_3r,
     sem_ls, sem_lr, sem_g3s, sem_g3r, sem_g2s, sem_g2r, sem_g1s, sem_g1r, sem_g0s, sem_g0r,
 ):
     rows, width = qx_ref.shape
@@ -267,26 +266,26 @@
     acc[...] = (grads[core] + half_recv[...]).reshape(acc.shape)
     pending.append(copy)
     loss_sum(base, copies)
-    base, copies = loss_round([by_mid])
-    for k in range(parts):
-        sendb[k] = acc[k, 1 - mid].astype(BF16)
-    copy = send(sendb, recvb, sem_bs.at[0], sem_br.at[0], by_mid)
-    copy.wait_recv()
-    pending.append(copy)
-    for k in range(parts):
-        accb[k] = acc[k, mid] + recvb[k].astype(F32)
-    loss_sum(base, copies)
-    base, copies = loss_round([by_part(k) for k in range(1, parts)])
     moved = []
     for k in range(1, parts):
-        sendc[k] = accb[lax.rem(part + k, parts)].astype(BF16)
-        moved.append(send(sendc.at[k], recvc.at[k], sem_cs.at[k], sem_cr.at[k], by_part(k)))
-    value = accb[part]
+        send1[k] = acc[lax.rem(part + k, parts)].astype(BF16)
+        moved.append(send(send1.at[k], recv1.at[k], sem_1s.at[k], sem_1r.at[k], by_part(k)))
+    base, copies = loss_round([by_part(k) for k in range(1, parts)])
+    value = acc[part]
     for k in range(1, parts):
         moved[k - 1].wait_recv()
-        value += recvc[k].astype(F32)
-    acc2[...] = value
+        value += recv1[k].astype(F32)
+    acc1[...] = value.reshape(acc1.shape)
     pending.extend(moved)
+    loss_sum(base, copies)
+
+    send2[...] = acc1[1 - mid].astype(BF16)
+    copy = send(send2, recv2, sem_2s.at[0], sem_2r.at[0], by_mid)
+    base, copies = loss_round([by_mid])
+    copy.wait_recv()
+    acc2[...] = (acc1[mid] + recv2[...].astype(F32)).reshape(acc2.shape)
+    pending.append(copy)
+    loss_sum(base, copies)
 
     moved = []
     for k in range(1, high):
@@ -298,7 +297,6 @@
         value += recv3[k].astype(F32)
     full[core, part, mid, hi] = value.astype(BF16)
     pending.extend(moved)
-    loss_sum(base, copies)
 
     place = full.at[core, part, mid, hi]
     moved = [send(place, place, sem_g3s.at[k], sem_g3r.at[k], by_high(k)) for k in range(1, high)]
@@ -345,7 +343,7 @@
     vmem, dma = pltpu.VMEM, pltpu.SemaphoreType.DMA
     block = (rows, embed)
     far = (2, high, r3, embed)
-    wide = (parts, high, r3, embed)
+    r1, r2 = width // parts, width // (2 * parts)
     scratch = [
         vmem((rows, width), BF16), vmem((rows, width), BF16),
         vmem((width, embed), BF16), vmem((width, embed), BF16),
@@ -357,17 +355,16 @@
         vmem((high, stat_rows, rows), F32),
         vmem((high, embed, rows), BF16), vmem((high, embed, rows), BF16), vmem((embed, rows), F32),
         vmem((LOW,) + block, BF16), vmem((LOW,) + block, BF16), vmem(block, F32), vmem(block, F32),
-        vmem((2, width, embed), F32), vmem((width, embed), F32), vmem((parts,) + far, F32),
-        vmem(far[1:], F32),
+        vmem((2, width, embed), F32), vmem((width, embed), F32), vmem((parts, r1, embed), F32),
+        vmem((parts, r1, embed), BF16), vmem((parts, r1, embed), BF16), vmem((2, r2, embed), F32),
+        vmem((r2, embed), BF16), vmem((r2, embed), BF16), vmem(far[1:], F32),
         vmem((high, r3, embed), BF16), vmem((high, r3, embed), BF16),
-        vmem(wide, BF16), vmem(wide, BF16), vmem(wide, F32), vmem(wide, BF16), vmem(wide, BF16),
         vmem((2, parts) + far, BF16), vmem((rounds, 8, LANES), F32),
     ]
     scratch += [dma((n,)) for n in (4, 2)]
     scratch += [dma((n,)) for n in (high, high, LOW, LOW, high, high, LOW, LOW)]
     scratch += [dma((n,)) for n in (high, high, high, high, LOW, LOW)]
-    scratch += [dma((n,)) for n in (1, 1, high, high)]
-    scratch += [dma((n,)) for n in (1, 1, parts, parts)]
+    scratch += [dma((n,)) for n in (1, 1, parts, parts, 1, 1, high, high)]
     scratch += [dma((n,)) for n in (rounds, rounds, high, high, parts, parts, parts, parts, 1, 1)]
     space = pltpu.VMEM
     grad, loss = pl.pallas_call(

time: 85.8 us -> 85.8 us (level)
  no operation moved by 1% of the time
where the time goes in v4:
time: 85.8 us; the launch traced here: 85.6 us
  Pallas kernels  80.4 us (94%)
  local copies, waits for them, and re-layouts  2.78 us (3%)
  between operations  2.4 us (3%)
    pallas_call x1, Pallas kernels, on_device(): pl.pallas_call(functools.partial(kernel, high, parts), out_shape=(jax.Sha...  80.4 us
    slice x1, local copies, waits for them, and re-layouts, on_device(): return (grad[0], grad[1], loss.reshape(()))  2.78 us

profile of v4, /device:TPU:1, one launch (start us, length us, event | category | flops | bytes accessed | tf_op | source)
XLA Modules:
  0.0 85.6 jit_solution(18443249501244105335)
XLA Ops:
  0.6 80.4 %two_tower.1 = (bf16[2,2,2,4,64,256]{5,4,3,2,1,0:T(8,128)(2,1)}, f32[1,1]{1,0:T(1,128)}) custom-call(bf16[384,1024]{1,0:T(8,128)(2,1)} %bitcast.8, bf16[384,1024]{1,0:T(8,128)(2,1)} %bitcast.9, s32[1,384]{1,0:T(1,128)} %ids_ref.1, s32[1,384]{1,0:T(1,128)} %buckets_ref.1, f32[1,256]{1,0:T(1,128)} %bitcast.10, bf16[1024,256]{1,0:T(8,128)(2,1)} %qw_hbm.1, ...), custom_call_target="tpu_custom_call" | custom-call | tf_op jit(solution)/shard_map/two_tower/pallas_call | solution.py:370
  81.0 2.8 %fusion = (f32[1,2,2,4,64,256]{5,4,3,2,1,0:T(8,128)}, f32[1,2,2,4,64,256]{5,4,3,2,1,0:T(8,128)}) fusion(bf16[2,2,2,4,64,256]{5,4,3,2,1,0:T(8,128)(2,1)} %get-tuple-element.5), kind=kLoop, calls=%fused_computation | loop fusion | bytes 4194304 | tf_op jit(solution)/shard_map/slice | solution.py:390
